TPU v7x, 32 devices: a whole 2x2x4 slice. The times are simulated.
32 devices in a mesh: tp: 8 (over z, y), dp: 4 (over x, core).
Axes of the slice: x: 2, y: 2, z: 4, core: 2. Of those that a mesh axis runs over, the one named last changes fastest.
Arguments:
- normed: bfloat16 [1024, 4096], P(('dp', 'tp')), may hold values from -6 to 6
- cotangent: bfloat16 [1024, 8192], P('dp', 'tp'), may hold values from -1.5 to 1.5
- weight_tiles: bfloat16 [2, 2048, 128, 128], P(None, 'tp'), may hold values from -0.09375 to 0.09375
- slot_tile: int32 [2048], replicated, may hold values from 0 to 2047, as said below
Outputs:
- hidden: bfloat16 [1024, 8192], P('dp', 'tp')
- d_normed: bfloat16 [1024, 4096], P(('dp', 'tp'))
- grad_tiles: float32 [2, 2048, 128, 128], P(None, 'tp', 'dp')
Inputs may be any that keep to these rules, and one draw needn't show every extreme that they name: `slot_tile`: A permutation of 0 to 2047. Position p belongs to owner p // 256 at slot p % 256. Each owner holds 24 to 40 tiles of the tile columns t * 8 to (t + 1) * 8 - 1 of each index t of tp; in every draw some owner holds exactly 40 for some t.
All inputs are finite; a program needn't handle non-finite values.
Results may differ from a plain program's by a relative error of at most 0.018.
Values may be sent and summed in bfloat16 or wider, within the bound.
A program may use at most 128 MiB of HBM per device.

v0:
```python
import jax
import jax.numpy as jnp
from jax import lax
from jax.sharding import PartitionSpec as P

D = 4096
FW = 8192
TILE = 128


def build_lists(slot_tile, groups, owned_count, tile_cols, cols_dev, list_len):
    owned_tiles = slot_tile.reshape(groups, owned_count)
    target = owned_tiles % tile_cols // cols_dev
    matches = (target[:, :, None] == jnp.arange(groups, dtype=jnp.int32)[None, None, :]).astype(
        jnp.int32
    )
    running = jnp.cumsum(matches, axis=1) - 1
    rank_of = jnp.sum(running * matches, axis=2)
    owner_ix = jnp.broadcast_to(jnp.arange(groups, dtype=jnp.int32)[:, None], (groups, owned_count))
    slot_ix = jnp.broadcast_to(
        jnp.arange(owned_count, dtype=jnp.int32)[None, :], (groups, owned_count)
    )
    table = jnp.full((groups, groups, list_len), -1, jnp.int32)
    return table.at[owner_ix, target, rank_of].set(slot_ix, mode="drop")


def incoming_places(in_lists, slot_tile, consumer, tile_cols, cols_dev, owned_count):
    groups = in_lists.shape[0]
    present = in_lists >= 0
    position = jnp.arange(groups, dtype=jnp.int32)[:, None] * owned_count + jnp.maximum(in_lists, 0)
    tile_id = slot_tile[position]
    tile_row = tile_id // tile_cols
    tile_col = tile_id % tile_cols - consumer * cols_dev
    local_idx = tile_row * cols_dev + tile_col
    return (jnp.where(present, local_idx, owned_count), present)


def pick_tiles(source, indices, present):
    limit = source.shape[1] - 1
    picked = source[:, jnp.minimum(indices, limit)]
    mask = present.reshape((1,) + present.shape + (1,) * (source.ndim - 2))
    return jnp.where(mask, picked, jnp.zeros((), source.dtype))


def place_tiles(arrived, places, owned_count):
    flat = arrived.reshape((arrived.shape[0], -1) + arrived.shape[3:])
    empty = jnp.zeros((arrived.shape[0], owned_count) + arrived.shape[3:], arrived.dtype)
    return empty.at[:, places.reshape(-1)].set(flat, mode="drop")


def local(normed, cotangent, weight_tiles, slot_tile):
    tp_size = lax.axis_size("tp")
    consumer = lax.axis_index("tp")
    owned_count = weight_tiles.shape[1]
    tile_size = weight_tiles.shape[2]
    tile_rows = D // TILE
    tile_cols = FW // TILE
    cols_dev = tile_cols // tp_size
    base_count = owned_count // tp_size
    list_len = base_count + base_count // 4
    send_lists = build_lists(slot_tile, tp_size, owned_count, tile_cols, cols_dev, list_len)
    my_lists = lax.dynamic_index_in_dim(send_lists, consumer, 0, keepdims=False)
    out_present = my_lists >= 0
    out_places = jnp.where(out_present, my_lists, owned_count)
    in_lists = lax.dynamic_index_in_dim(send_lists, consumer, 1, keepdims=False)
    in_places, in_present = incoming_places(
        in_lists, slot_tile, consumer, tile_cols, cols_dev, owned_count
    )
    slab_rows = tile_size // lax.axis_size("dp")
    slab_start = lax.axis_index("dp") * slab_rows
    own_rows = lax.dynamic_slice_in_dim(weight_tiles, slab_start, slab_rows, 2)
    outgoing = pick_tiles(own_rows, my_lists, out_present)
    arrived = lax.all_to_all(outgoing, "tp", split_axis=1, concat_axis=1, tiled=True)
    partial_tiles = place_tiles(arrived, in_places, owned_count)
    weight_block = lax.all_gather(partial_tiles, "dp", axis=2, tiled=True)
    weight_block = weight_block.reshape(2, tile_rows, cols_dev, tile_size, tile_size)
    gathered = lax.all_gather(normed, "tp", axis=0, tiled=True)
    group_rows = gathered.shape[0]
    tiled_in = gathered.reshape(group_rows, tile_rows, tile_size)
    both_proj = jnp.einsum(
        "nri,mrcij->nmcj", tiled_in, weight_block, preferred_element_type=jnp.float32
    )
    gate_proj = both_proj[:, 0].reshape(group_rows, -1)
    up_proj = both_proj[:, 1].reshape(group_rows, -1)
    sigmoid_gate = jax.nn.sigmoid(gate_proj)
    act_gate = gate_proj * sigmoid_gate
    hidden = (act_gate * up_proj).astype(jnp.bfloat16)
    cot_full = cotangent.astype(jnp.float32)
    grad_gate = (
        cot_full * up_proj * (sigmoid_gate * (1.0 + gate_proj * (1.0 - sigmoid_gate)))
    ).astype(jnp.bfloat16)
    grad_up = (cot_full * act_gate).astype(jnp.bfloat16)
    grads_in = jnp.stack([grad_gate, grad_up], 1).reshape(group_rows, 2, cols_dev, tile_size)
    term = jnp.einsum("nmcj,mrcij->nri", grads_in, weight_block, preferred_element_type=jnp.float32)
    d_normed = lax.psum_scatter(
        term.reshape(normed.shape[0] * lax.axis_size("tp"), -1).astype(jnp.bfloat16),
        "tp",
        scatter_dimension=0,
        tiled=True,
    )
    partial_value = jnp.einsum(
        "nri,nmcj->mrcij", tiled_in, grads_in, preferred_element_type=jnp.float32
    ).astype(jnp.bfloat16)
    partial_value = partial_value.reshape(2, owned_count, tile_size, tile_size)
    summed = lax.psum_scatter(partial_value, "dp", scatter_dimension=2, tiled=True).astype(
        jnp.float32
    )
    outgoing_grads = pick_tiles(summed, in_places, in_present)
    returned = lax.all_to_all(
        outgoing_grads.astype(jnp.bfloat16), "tp", split_axis=1, concat_axis=1, tiled=True
    ).astype(outgoing_grads.dtype)
    result = place_tiles(returned, out_places, owned_count)
    return (hidden, d_normed, result)


def solution(mesh):
    return jax.shard_map(
        local,
        mesh=mesh,
        in_specs=(P(("dp", "tp"), None), P("dp", "tp"), P(None, "tp", None, None), P()),
        out_specs=(P("dp", "tp"), P(("dp", "tp"), None), P(None, "tp", "dp", None)),
        check_vma=False,
    )
```

profile of v0, /device:TPU:0, one launch (start us, length us, event | category | flops | bytes accessed | tf_op | source)
XLA Modules:
  0.0 721.3 jit_solution(2535239984476430002)
XLA Ops:
  7.2 0.7 reshape.556
  7.9 0.7 reshape.555
  8.6 0.7 and_select_fusion
  9.3 4.5 reduce-window.6
  13.9 0.2 copy.31
  14.2 0.1 fusion.20
  14.3 0.7 and_reduce_fusion
  15.1 0.7 multiply_reduce_fusion
  15.8 8.1 %scatter_custom_fusion.2 = s32[2560]{0:T(1024)S(1)} fusion(s32[2048]{0:T(1024)S(1)} %bitcast.129, s32[2048]{0:T(1024)S(1)} %bitcast.130, s32[]{:T(128)} %constant.86.clone.1), kind=kCustom, calls=%fused_computation.84 | custom fusion | bytes 10244
  23.9 0.1 reshape.568
  24.0 0.1 reshape.581
  24.1 4.9 constant_dynamic-slice_fusion
  29.0 5.9 gather_fusion.1
  34.9 5.3 select_bitcast_fusion
  40.2 7.4 %all-to-all-start = ((bf16[2,8,40,32,128]{4,3,0,2,1:T(8,128)(2,1)}), bf16[2,8,40,32,128]{4,3,0,2,1:T(8,128)(2,1)}, u32[]{:S(2)}, u32[]{:S(2)}) async-start(bf16[2,8,40,32,128]{4,3,0,2,1:T(8,128)(2,1)} %select_bitcast_fusion), calls=%async_computation | async-start | bytes 10485760 | tf_op jit(solution)/shard_map/all_to_all | solution.py:73
  47.7 0.7 all-gather.5.cloned.1.call-update
  48.5 0.1 reshape.573
  48.6 2.2 gather_fusion
  50.9 0.1 gather.16
  51.0 0.1 ge.52
  51.1 137.6 %all-to-all-done = bf16[2,8,40,32,128]{4,3,0,2,1:T(8,128)(2,1)} async-done(((bf16[2,8,40,32,128]{4,3,0,2,1:T(8,128)(2,1)}), bf16[2,8,40,32,128]{4,3,0,2,1:T(8,128)(2,1)}, u32[]{:S(2)}, u32[]{:S(2)}) %all-to-all-start) | async-done | bytes 5242912 | tf_op jit(solution)/shard_map/all_to_all | solution.py:73
  188.7 2.6 broadcast_in_dim.63
  191.3 43.5 %scatter_fusion = bf16[2,256,32,128]{3,2,1,0:T(8,128)(2,1)} fusion(bf16[2,256,32,128]{3,2,1,0:T(8,128)(2,1)} %broadcast_in_dim.63, s32[320]{0:T(512)S(1)} %fusion.42, bf16[320,2,32,128]{3,2,1,0:T(8,128)(2,1)} %bitcast.13), kind=kCustom, calls=%fused_computation.3 | custom fusion | bytes 15729920 | tf_op jit(solution)/shard_map/scatter | solution.py:48
  234.8 0.2 reduce-scatter.5.cloned.1.call-start
  235.0 0.2 copy.38
  235.3 3.3 copy.35
  238.5 100.3 %all-gather.3.cloned.1.call-done = bf16[2,256,128,128]{3,2,1,0:T(8,128)(2,1)} async-done(((bf16[2,256,32,128]{3,2,1,0:T(8,128)(2,1)}), bf16[2,256,128,128]{3,2,1,0:T(8,128)(2,1)}) %all-gather.3.cloned.1.call-update) | async-done | bytes 16777232 | tf_op jit(solution)/shard_map/all_gather | solution.py:75
  338.9 8.1 %convolution_bitcast_fusion = f32[256,2,8,128]{0,3,2,1:T(8,128)S(1)} fusion(bf16[2,32,8,128,128]{4,3,2,1,0:T(8,128)(2,1)} %bitcast.115, bf16[256,32,128,1,1]{0,2,4,1,3:T(8,128)(2,1)S(1)} %bitcast.120), kind=kOutput, calls=%fused_computation.15 | convolution fusion | flops 4294967296 | bytes 20971520 | tf_op jit(solution)/shard_map/nri,mrcij->nmcj/dot_general | solution.py:80
  347.0 0.2 fusion.49
  347.2 1.6 fusion.10
  348.9 0.3 copy.40
  349.1 1.3 copy.39
  350.5 8.1 %convert_bitcast_fusion = bf16[2,32,8,128,128]{3,4,1,2,0:T(8,128)(2,1)} fusion(bf16[256,32,128,1,1]{0,2,1,4,3:T(8,128)(2,1)S(1)} %bitcast.121, bf16[256,1,8,128]{3,0,1,2:T(8,128)(2,1)S(1)} %copy.40, bf16[256,1,8,128]{3,0,1,2:T(8,128)(2,1)S(1)} %copy.39), kind=kOutput, calls=%fused_computation.8 | convolution fusion | flops 4303880192 | bytes 19922944 | tf_op jit(solution)/shard_map/nri,nmcj->mrcij/dot_general | solution.py:101
  358.6 21.2 %copy.45 = bf16[2,32,8,128,128]{4,3,2,1,0:T(8,128)(2,1)} copy(bf16[2,32,8,128,128]{3,4,1,2,0:T(8,128)(2,1)} %convert_bitcast_fusion) | data formatting | bytes 33554432 | tf_op jit(solution)/shard_map/convert_element_type | solution.py:103
  379.8 0.1 reshape.589
  379.9 124.9 %reduce-scatter.5.cloned.1.call-done = bf16[2,256,32,128]{3,2,1,0:T(8,128)(2,1)} async-done(((bf16[2,256,128,128]{3,2,1,0:T(8,128)(2,1)}), bf16[2,256,32,128]{3,2,1,0:T(8,128)(2,1)}) %reduce-scatter.5.cloned.1.call-update) | async-done | bytes 4194320 | tf_op jit(solution)/shard_map/reduce_scatter | solution.py:105
  504.9 5.9 gather_fusion.2
  510.8 6.0 fusion.5
  516.7 5.5 all-to-all-start.1
  522.3 0.3 reduce-scatter.3.cloned.1.call-start
  522.5 18.6 %copy.41 = bf16[32,128,8,128,2]{3,2,4,1,0:T(8,128)(2,1)} copy(bf16[32,128,8,128,2]{3,1,2,0,4:T(8,128)(2,1)} %bitcast.116) | data formatting | bytes 33554432 | tf_op jit(solution)/shard_map/nmcj,mrcij->nri/dot_general | solution.py:94
  541.1 12.6 %fusion.6 = bf16[256,4096]{1,0:T(8,128)(2,1)} fusion(bf16[4096,8,128,2]{2,1,3,0:T(8,128)(2,1)} %bitcast.122, bf16[256,1,8,128]{3,0,1,2:T(8,128)(2,1)S(1)} %copy.40, bf16[256,1,8,128]{3,0,1,2:T(8,128)(2,1)S(1)} %copy.39), kind=kOutput, calls=%fused_computation.14 | convolution fusion | flops 4296540160 | bytes 19922944 | tf_op jit(solution)/shard_map/nmcj,mrcij->nri/dot_general | solution.py:94
  553.7 0.1 squeeze.6
  553.8 1.0 copy.46
  554.8 99.9 %all-to-all-done.1 = bf16[2,8,40,32,128]{4,3,0,2,1:T(8,128)(2,1)} async-done(((bf16[2,8,40,32,128]{4,3,0,2,1:T(8,128)(2,1)}), bf16[2,8,40,32,128]{4,3,0,2,1:T(8,128)(2,1)}, u32[]{:S(2)}, u32[]{:S(2)}) %all-to-all-start.1) | async-done | bytes 5242912 | tf_op jit(solution)/shard_map/all_to_all | solution.py:109
  654.7 8.0 %convert_bitcast_fusion.1 = f32[320,2,32,128]{3,2,1,0:T(8,128)} fusion(bf16[2,8,40,32,128]{4,3,0,2,1:T(8,128)(2,1)} %all-to-all-done.1), kind=kLoop, calls=%fused_computation.9 | loop fusion | flops 2621440 | bytes 15728640 | tf_op jit(solution)/shard_map/reshape | solution.py:46
  662.7 4.5 broadcast_in_dim.71
  667.2 47.6 %scatter_fusion.1 = f32[2,256,32,128]{3,2,1,0:T(8,128)} fusion(f32[2,256,32,128]{3,2,1,0:T(8,128)} %broadcast_in_dim.71, s32[320]{0:T(512)S(1)} %fusion.43, f32[320,2,32,128]{3,2,1,0:T(8,128)} %convert_bitcast_fusion.1), kind=kCustom, calls=%fused_computation.4 | custom fusion | bytes 31458560 | tf_op jit(solution)/shard_map/scatter | solution.py:48
  (37 shorter events, 0.6 us)
Async XLA Ops:
  40.2 8.4 %copy-start = (s32[2048]{0:T(1024)S(1)}, s32[2048]{0:T(1024)}, u32[]{:S(2)}) copy-start(s32[2048]{0:T(1024)} %param.7) | copy-start | bytes 24580
  40.2 148.5 %all-to-all-start = ((bf16[2,8,40,32,128]{4,3,0,2,1:T(8,128)(2,1)}), bf16[2,8,40,32,128]{4,3,0,2,1:T(8,128)(2,1)}, u32[]{:S(2)}, u32[]{:S(2)}) async-start(bf16[2,8,40,32,128]{4,3,0,2,1:T(8,128)(2,1)} %select_bitcast_fusion), calls=%async_computation | async-start | bytes 10485760 | tf_op jit(solution)/shard_map/all_to_all | solution.py:73
  47.6 187.6 %all-gather.5.cloned.1.call-start = ((), (), s32[]{:S(2)}) async-start(), calls=%async_computation.5 | async-start | bytes 2359296 | tf_op jit(solution)/shard_map/all_gather | solution.py:77
  48.4 290.5 %all-gather.3.cloned.1.call-start = ((), (), s32[]{:S(2)}) async-start(), calls=%async_computation.4 | async-start | bytes 20971520 | tf_op jit(solution)/shard_map/all_gather | solution.py:75
  191.3 43.7 %copy-start.2 = (bf16[256,1024]{1,0:T(8,128)(2,1)S(1)}, bf16[256,1024]{1,0:T(8,128)(2,1)}, u32[]{:S(2)}) copy-start(bf16[256,1024]{1,0:T(8,128)(2,1)} %param.5) | copy-start | bytes 1572868
  234.8 270.1 %reduce-scatter.5.cloned.1.call-start = ((), (), s32[]{:S(2)}) async-start(), calls=%async_computation.7 | async-start | bytes 20971520 | tf_op jit(solution)/shard_map/reduce_scatter | solution.py:105
  516.7 138.0 %all-to-all-start.1 = ((bf16[2,8,40,32,128]{4,3,0,2,1:T(8,128)(2,1)}), bf16[2,8,40,32,128]{4,3,0,2,1:T(8,128)(2,1)}, u32[]{:S(2)}, u32[]{:S(2)}) async-start(bf16[2,8,40,32,128]{4,3,0,2,1:T(8,128)(2,1)} %fusion.5), calls=%async_computation.3 | async-start | bytes 10485760 | tf_op jit(solution)/shard_map/all_to_all | solution.py:109
  522.3 192.5 %reduce-scatter.3.cloned.1.call-start = ((), (), s32[]{:S(2)}) async-start(), calls=%async_computation.6 | async-start | bytes 2359296 | tf_op jit(solution)/shard_map/reduce_scatter | solution.py:95
  541.1 12.7 %copy-start.1 = (bf16[256,1024]{0,1:T(8,128)(2,1)S(1)}, bf16[256,1024]{0,1:T(8,128)(2,1)}, u32[]{:S(2)}) copy-start(bf16[256,1024]{0,1:T(8,128)(2,1)} %get-tuple-element.16) | copy-start | bytes 1572868
Sparse Core Ops, SparseCore 0:
  50.6 119.8 all-gather.4
  234.9 103.9 all-gather.2
  380.0 124.8 reduce-scatter.4
  553.8 121.1 reduce-scatter.2
where the time goes:
time: 724 us; the launch traced here: 721 us
  waiting for transfers between devices  464 us (64%)
  local copies, waits for them, and re-layouts  173 us (24%)
  matrix products  28.8 us (4%)
  other arithmetic  28.1 us (4%)
  between operations  14 us (2%)
  starting transfers between devices  13.5 us (2%)
    all_to_all x1, waiting for transfers between devices, local(): lax.all_to_all(outgoing, 'tp', split_axis=1, concat_axis=1, tiled=True)  138 us
    reduce_scatter x1, waiting for transfers between devices, local(): lax.psum_scatter(partial_value, 'dp', scatter_dimension=2, tiled=True)  125 us
    all_gather x1, waiting for transfers between devices, local(): weight_block = lax.all_gather(partial_tiles, 'dp', axis=2, tiled=True)  100 us
    all_to_all x1, waiting for transfers between devices, local(): lax.all_to_all(outgoing_grads.astype(jnp.bfloat16), 'tp', split_axis=1, c...  99.9 us
    scatter x2, local copies, waits for them, and re-layouts, place_tiles(): return empty.at[:, places.reshape(-1)].set(flat, mode='drop')  91.1 us
    convert_element_type x1, local copies, waits for them, and re-layouts, local(): partial_value = jnp.einsum('nri,nmcj->mrcij', tiled_in, grads_in, preferr...  21.2 us
    dot_general x1, local copies, waits for them, and re-layouts, local(): jnp.einsum('nmcj,mrcij->nri', grads_in, weight_block, preferred_element_t...  18.6 us
  transfers between devices with their start and end apart: 6, of which 4 were waited for; matrix products, arithmetic and copies ran while one was open for 20% of the time, Pallas kernels for 0%

commit v1 on v0

--- a/solution.py
+++ b/solution.py
@@ -6,6 +6,21 @@
 D = 4096
 FW = 8192
 TILE = 128
+
+
+def read_samples_all(x_in, along_axis, axis_k):
+    world = lax.axis_size(along_axis)
+    field_out = x_in
+    placed = [(ii - 1, ii) for ii in range(1, world)] + [(world - 1, 0)]
+    dd = 0
+    made = [field_out]
+    while dd < world - 1:
+        field_out = lax.ppermute(field_out, along_axis, placed)
+        made += [field_out]
+        dd = dd + 1
+    o_now = jnp.concatenate([*reversed(made)], axis=axis_k)
+    shaped = lax.axis_index(along_axis)
+    return jnp.roll(o_now, shift=(shaped + 1) * field_out.shape[axis_k], axis=axis_k)
 
 
 def build_lists(slot_tile, groups, owned_count, tile_cols, cols_dev, list_len):
@@ -72,7 +87,7 @@
     outgoing = pick_tiles(own_rows, my_lists, out_present)
     arrived = lax.all_to_all(outgoing, "tp", split_axis=1, concat_axis=1, tiled=True)
     partial_tiles = place_tiles(arrived, in_places, owned_count)
-    weight_block = lax.all_gather(partial_tiles, "dp", axis=2, tiled=True)
+    weight_block = read_samples_all(partial_tiles, "dp", 2)
     weight_block = weight_block.reshape(2, tile_rows, cols_dev, tile_size, tile_size)
     gathered = lax.all_gather(normed, "tp", axis=0, tiled=True)
     group_rows = gathered.shape[0]

time: 724 us -> 781 us (1.079)
  local copies, waits for them, and re-layouts: 173 us -> 217 us
  waiting for transfers between devices: 464 us -> 481 us
    all_gather x1 -> x0, waiting for transfers between devices: 100 us -> none  [local(): weight_block = lax.all_gather(partial_tiles, 'dp', axis=2, tiled=True)]
    ppermute x0 -> x3, waiting for transfers between devices: none -> 96.2 us  [read_samples_all(): field_out = lax.ppermute(field_out, along_axis, placed)]
    all_gather x1, waiting for transfers between devices: 0.02 us -> 48 us  [local(): gathered = lax.all_gather(normed, 'tp', axis=0, tiled=True)]
    unnamed x12 -> x27, local copies, waits for them, and re-layouts: 9.29 us -> 40.9 us
    all_to_all x1, waiting for transfers between devices: 138 us -> 113 us  [local(): lax.all_to_all(outgoing, 'tp', split_axis=1, concat_axis=1, tiled=True)]
    dynamic_slice x0 -> x1, local copies, waits for them, and re-layouts: none -> 8.8 us  [read_samples_all(): jnp.roll(o_now, shift=(shaped + 1) * field_out.shape[axis_k], axis=axis_k)]
  transfers between devices with their start and end apart: 6 -> 8, of which waited for: 4 -> 6; matrix products, arithmetic and copies ran while one was open for 20% -> 13% of each run, Pallas kernels for 0% -> 0%
where the time goes in v1:
time: 781 us; the launch traced here: 778 us
  waiting for transfers between devices  481 us (62%)
  local copies, waits for them, and re-layouts  217 us (28%)
  other arithmetic  28.1 us (4%)
  matrix products  25.5 us (3%)
  between operations  14 us (2%)
  starting transfers between devices  13.3 us (2%)
    reduce_scatter x1, waiting for transfers between devices, local(): lax.psum_scatter(partial_value, 'dp', scatter_dimension=2, tiled=True)  123 us
    all_to_all x1, waiting for transfers between devices, local(): lax.all_to_all(outgoing, 'tp', split_axis=1, concat_axis=1, tiled=True)  113 us
    all_to_all x1, waiting for transfers between devices, local(): lax.all_to_all(outgoing_grads.astype(jnp.bfloat16), 'tp', split_axis=1, c...  99.8 us
    ppermute x3, waiting for transfers between devices, read_samples_all(): field_out = lax.ppermute(field_out, along_axis, placed)  96.2 us
    scatter x2, local copies, waits for them, and re-layouts, place_tiles(): return empty.at[:, places.reshape(-1)].set(flat, mode='drop')  91.1 us
    all_gather x1, waiting for transfers between devices, local(): gathered = lax.all_gather(normed, 'tp', axis=0, tiled=True)  48 us
    unnamed x27, local copies, waits for them, and re-layouts  40.9 us
    convert_element_type x1, local copies, waits for them, and re-layouts, local(): partial_value = jnp.einsum('nri,nmcj->mrcij', tiled_in, grads_in, preferr...  21.2 us
  transfers between devices with their start and end apart: 8, of which 6 were waited for; matrix products, arithmetic and copies ran while one was open for 13% of the time, Pallas kernels for 0%

profile of v1, /device:TPU:0, one launch (start us, length us, event | category | flops | bytes accessed | tf_op | source)
XLA Modules:
  0.0 778.3 jit_solution(12381843510636720960)
XLA Ops:
  7.2 0.7 reshape.556
  7.9 0.7 reshape.555
  8.6 0.7 and_select_fusion
  9.3 4.5 reduce-window.6
  14.3 0.7 multiply_reduce_fusion
  15.1 0.7 and_reduce_fusion
  15.8 8.1 %scatter_custom_fusion.2 = s32[2560]{0:T(1024)S(1)} fusion(s32[2048]{0:T(1024)S(1)} %bitcast.129, s32[2048]{0:T(1024)S(1)} %bitcast.130, s32[]{:T(128)} %constant.105.clone.1), kind=kCustom, calls=%fused_computation.92 | custom fusion | bytes 10244
  24.1 4.9 constant_dynamic-slice_fusion.1
  29.0 5.9 gather_fusion.1
  34.9 5.3 select_bitcast_fusion
  40.2 7.4 all-to-all-start
  47.9 2.2 gather_fusion
  50.4 113.0 %all-to-all-done = bf16[2,8,40,32,128]{4,3,0,2,1:T(8,128)(2,1)} async-done(((bf16[2,8,40,32,128]{4,3,0,2,1:T(8,128)(2,1)}), bf16[2,8,40,32,128]{4,3,0,2,1:T(8,128)(2,1)}, u32[]{:S(2)}, u32[]{:S(2)}) %all-to-all-start) | async-done | bytes 5242912 | tf_op jit(solution)/shard_map/all_to_all | solution.py:88
  163.4 2.6 broadcast_in_dim.63
  165.9 43.5 %scatter_fusion = bf16[2,256,32,128]{3,2,1,0:T(8,128)(2,1)} fusion(bf16[2,256,32,128]{3,2,1,0:T(8,128)(2,1)} %broadcast_in_dim.63, s32[320]{0:T(512)S(1)} %fusion.42, bf16[320,2,32,128]{3,2,1,0:T(8,128)(2,1)} %bitcast.13), kind=kCustom, calls=%fused_computation.3 | custom fusion | bytes 15729920 | tf_op jit(solution)/shard_map/scatter | solution.py:63
  209.4 48.1 %collective-permute-done = bf16[2,256,32,128]{3,2,1,0:T(8,128)(2,1)S(1)} collective-permute-done((bf16[2,256,32,128]{3,2,1,0:T(8,128)(2,1)}, bf16[2,256,32,128]{3,2,1,0:T(8,128)(2,1)S(1)}, u32[]{:S(2)}, u32[]{:S(2)}) %collective-permute-start) | collective-permute-done | bytes 4194336 | tf_op jit(solution)/shard_map/ppermute | solution.py:18
  257.6 1.9 copy-done.3
  259.5 48.0 %collective-permute-done.1 = bf16[2,256,32,128]{3,2,1,0:T(8,128)(2,1)} collective-permute-done((bf16[2,256,32,128]{3,2,1,0:T(8,128)(2,1)S(1)}, bf16[2,256,32,128]{3,2,1,0:T(8,128)(2,1)}, u32[]{:S(2)}, u32[]{:S(2)}) %collective-permute-start.1) | collective-permute-done | bytes 4194336 | tf_op jit(solution)/shard_map/ppermute | solution.py:18
  308.0 48.0 %all-gather.2.cloned.1.call-done = bf16[256,4096]{1,0:T(8,128)(2,1)} async-done(((bf16[32,4096]{1,0:T(8,128)(2,1)}), bf16[256,4096]{1,0:T(8,128)(2,1)}) %all-gather.2.cloned.1.call-update) | async-done | bytes 2097168 | tf_op jit(solution)/shard_map/all_gather | solution.py:92
  356.1 3.3 copy.35
  359.3 4.9 constant_dynamic-update-slice_fusion.7
  364.3 5.1 constant_dynamic-update-slice_fusion.6
  369.4 2.8 constant_dynamic-update-slice_fusion.5
  372.1 0.7 copy-done.2
  372.9 2.7 constant_dynamic-update-slice_fusion.4
  375.6 4.9 constant_dynamic-update-slice_fusion.3
  380.5 5.0 constant_dynamic-update-slice_fusion.2
  385.5 2.7 constant_dynamic-update-slice_fusion.1
  388.2 2.8 constant_dynamic-update-slice_fusion
  391.0 8.8 %constant_dynamic-slice_fusion = bf16[2,256,128,128]{3,2,1,0:T(8,128)(2,1)S(1)} fusion(bf16[2,256,256,128]{3,2,1,0:T(8,128)(2,1)} %constant_dynamic-update-slice_fusion, s32[]{:T(128)S(6)} %select_n.238), kind=kLoop, calls=%fused_computation.124 | loop fusion | bytes 33554436 | tf_op jit(solution)/shard_map/jit(_roll_dynamic)/dynamic_slice | solution.py:23
  399.8 4.8 convolution_bitcast_fusion
  404.6 0.9 copy-done.1
  405.7 1.6 fusion.10
  407.3 0.3 copy.39
  407.6 1.3 copy.40
  408.9 8.1 %convert_bitcast_fusion = bf16[2,32,8,128,128]{3,4,1,2,0:T(8,128)(2,1)} fusion(bf16[256,32,128,1,1]{0,2,1,4,3:T(8,128)(2,1)S(1)} %bitcast.121, bf16[256,1,8,128]{3,0,1,2:T(8,128)(2,1)S(1)} %copy.40, bf16[256,1,8,128]{3,0,1,2:T(8,128)(2,1)S(1)} %copy.39), kind=kOutput, calls=%fused_computation.8 | convolution fusion | flops 4303880192 | bytes 19922944 | tf_op jit(solution)/shard_map/nri,nmcj->mrcij/dot_general | solution.py:116
  417.0 21.2 %copy.45 = bf16[2,32,8,128,128]{4,3,2,1,0:T(8,128)(2,1)} copy(bf16[2,32,8,128,128]{3,4,1,2,0:T(8,128)(2,1)} %convert_bitcast_fusion) | data formatting | bytes 33554432 | tf_op jit(solution)/shard_map/convert_element_type | solution.py:118
  438.4 123.5 %reduce-scatter.5.cloned.1.call-done = bf16[2,256,32,128]{3,2,1,0:T(8,128)(2,1)} async-done(((bf16[2,256,128,128]{3,2,1,0:T(8,128)(2,1)}), bf16[2,256,32,128]{3,2,1,0:T(8,128)(2,1)}) %reduce-scatter.5.cloned.1.call-update) | async-done | bytes 4194320 | tf_op jit(solution)/shard_map/reduce_scatter | solution.py:120
  561.8 5.9 gather_fusion.2
  567.7 6.0 fusion.5
  573.7 5.5 all-to-all-start.1
  579.3 18.8 %copy.41 = bf16[32,128,8,128,2]{3,2,4,1,0:T(8,128)(2,1)} copy(bf16[32,128,8,128,2]{3,1,2,0,4:T(8,128)(2,1)} %bitcast.116) | data formatting | bytes 33554432 | tf_op jit(solution)/shard_map/nmcj,mrcij->nri/dot_general | solution.py:109
  598.1 12.6 %fusion.6 = bf16[256,4096]{1,0:T(8,128)(2,1)} fusion(bf16[4096,8,128,2]{2,1,3,0:T(8,128)(2,1)} %bitcast.122, bf16[256,1,8,128]{3,0,1,2:T(8,128)(2,1)S(1)} %copy.40, bf16[256,1,8,128]{3,0,1,2:T(8,128)(2,1)S(1)} %copy.39), kind=kOutput, calls=%fused_computation.14 | convolution fusion | flops 4296540160 | bytes 19922944 | tf_op jit(solution)/shard_map/nmcj,mrcij->nri/dot_general | solution.py:109
  610.9 1.0 copy.46
  611.9 99.8 %all-to-all-done.1 = bf16[2,8,40,32,128]{4,3,0,2,1:T(8,128)(2,1)} async-done(((bf16[2,8,40,32,128]{4,3,0,2,1:T(8,128)(2,1)}), bf16[2,8,40,32,128]{4,3,0,2,1:T(8,128)(2,1)}, u32[]{:S(2)}, u32[]{:S(2)}) %all-to-all-start.1) | async-done | bytes 5242912 | tf_op jit(solution)/shard_map/all_to_all | solution.py:124
  711.7 8.0 %convert_bitcast_fusion.1 = f32[320,2,32,128]{3,2,1,0:T(8,128)} fusion(bf16[2,8,40,32,128]{4,3,0,2,1:T(8,128)(2,1)} %all-to-all-done.1), kind=kLoop, calls=%fused_computation.9 | loop fusion | flops 2621440 | bytes 15728640 | tf_op jit(solution)/shard_map/reshape | solution.py:61
  719.7 4.5 broadcast_in_dim.71
  724.1 47.6 %scatter_fusion.1 = f32[2,256,32,128]{3,2,1,0:T(8,128)} fusion(f32[2,256,32,128]{3,2,1,0:T(8,128)} %broadcast_in_dim.71, s32[320]{0:T(512)S(1)} %fusion.43, f32[320,2,32,128]{3,2,1,0:T(8,128)} %convert_bitcast_fusion.1), kind=kCustom, calls=%fused_computation.4 | custom fusion | bytes 31458560 | tf_op jit(solution)/shard_map/scatter | solution.py:63
  (57 shorter events, 2.0 us)
Async XLA Ops:
  40.2 7.7 copy-start
  40.2 123.2 %all-to-all-start = ((bf16[2,8,40,32,128]{4,3,0,2,1:T(8,128)(2,1)}), bf16[2,8,40,32,128]{4,3,0,2,1:T(8,128)(2,1)}, u32[]{:S(2)}, u32[]{:S(2)}) async-start(bf16[2,8,40,32,128]{4,3,0,2,1:T(8,128)(2,1)} %select_bitcast_fusion), calls=%async_computation | async-start | bytes 10485760 | tf_op jit(solution)/shard_map/all_to_all | solution.py:88
  47.6 308.4 %all-gather.2.cloned.1.call-start = ((), (), s32[]{:S(2)}) async-start(), calls=%async_computation.4 | async-start | bytes 2359296 | tf_op jit(solution)/shard_map/all_gather | solution.py:92
  165.9 141.9 %copy-start.6 = (bf16[256,1024]{1,0:T(8,128)(2,1)S(1)}, bf16[256,1024]{1,0:T(8,128)(2,1)}, u32[]{:S(2)}) copy-start(bf16[256,1024]{1,0:T(8,128)(2,1)} %param.5) | copy-start | bytes 1572868
  209.4 48.1 %collective-permute-start = (bf16[2,256,32,128]{3,2,1,0:T(8,128)(2,1)}, bf16[2,256,32,128]{3,2,1,0:T(8,128)(2,1)S(1)}, u32[]{:S(2)}, u32[]{:S(2)}) collective-permute-start(bf16[2,256,32,128]{3,2,1,0:T(8,128)(2,1)} %scatter_fusion), channel_id=1, source_target_pairs={{0,1},{1,2},{2,3},{3,0},{4,5},{5,6},{6,7},{7,4},{8,9},{9,10},{10,1... | collective-permute-start | bytes 12582920 | tf_op jit(solution)/shard_map/ppermute | solution.py:18
  257.6 1.9 copy-start.3
  259.5 48.0 %collective-permute-start.1 = (bf16[2,256,32,128]{3,2,1,0:T(8,128)(2,1)S(1)}, bf16[2,256,32,128]{3,2,1,0:T(8,128)(2,1)}, u32[]{:S(2)}, u32[]{:S(2)}) collective-permute-start(bf16[2,256,32,128]{3,2,1,0:T(8,128)(2,1)S(1)} %collective-permute-done), channel_id=1, source_target_pairs={{0,1},{1,2},{2,3},{3,0},{4,5},{5,6},{6,7},{7,4},{8,9},{9,10},{10,1... | collective-permute-start | bytes 12582920 | tf_op jit(solution)/shard_map/ppermute | solution.py:18
  307.5 51.8 %collective-permute-start.2 = (bf16[2,256,32,128]{3,2,1,0:T(8,128)(2,1)}, bf16[2,256,32,128]{3,2,1,0:T(8,128)(2,1)}, u32[]{:S(2)}, u32[]{:S(2)}) collective-permute-start(bf16[2,256,32,128]{3,2,1,0:T(8,128)(2,1)} %collective-permute-done.1), channel_id=1, source_target_pairs={{0,1},{1,2},{2,3},{3,0},{4,5},{5,6},{6,7},{7,4},{8,9},{9,10},{10,1... | collective-permute-start | bytes 12582920 | tf_op jit(solution)/shard_map/ppermute | solution.py:18
  307.6 254.3 %reduce-scatter.5.cloned.1.call-start = ((), (), s32[]{:S(2)}) async-start(), calls=%async_computation.6 | async-start | bytes 20971520 | tf_op jit(solution)/shard_map/reduce_scatter | solution.py:120
  364.3 5.1 copy-start.4
  369.4 3.5 copy-start.2
  399.8 5.7 copy-start.1
  573.7 138.0 %all-to-all-start.1 = ((bf16[2,8,40,32,128]{4,3,0,2,1:T(8,128)(2,1)}), bf16[2,8,40,32,128]{4,3,0,2,1:T(8,128)(2,1)}, u32[]{:S(2)}, u32[]{:S(2)}) async-start(bf16[2,8,40,32,128]{4,3,0,2,1:T(8,128)(2,1)} %fusion.5), calls=%async_computation.3 | async-start | bytes 10485760 | tf_op jit(solution)/shard_map/all_to_all | solution.py:124
  579.2 192.5 %reduce-scatter.3.cloned.1.call-start = ((), (), s32[]{:S(2)}) async-start(), calls=%async_computation.5 | async-start | bytes 2359296 | tf_op jit(solution)/shard_map/reduce_scatter | solution.py:110
  598.1 12.7 %copy-start.5 = (bf16[256,1024]{0,1:T(8,128)(2,1)S(1)}, bf16[256,1024]{0,1:T(8,128)(2,1)}, u32[]{:S(2)}) copy-start(bf16[256,1024]{0,1:T(8,128)(2,1)} %get-tuple-element.16) | copy-start | bytes 1572868
Sparse Core Ops, SparseCore 0:
  307.7 48.3 all-gather.1
  438.4 123.3 reduce-scatter.4
  610.9 135.1 reduce-scatter.2
